TPU v7x, 32 devices: a whole 2x2x4 slice. The times are simulated.
32 devices in a mesh: pts: 8 (over z, core), head: 4 (over y, x).
Axes of the slice: x: 2, y: 2, z: 4, core: 2. Of those that a mesh axis runs over, the one named last changes fastest.
Arguments:
- points: bfloat16 [73728, 128], P('pts')
- counts: int32 [8], P('pts'), may hold values from 1 to 9216, 55296 in all
- ln1_gain: float32 [2, 128], replicated, may hold values from 0.5 to 1.5
- ln1_bias: float32 [2, 128], replicated, may hold values from -1.5 to 1.5
- w_in: bfloat16 [2, 128, 128], P(None, None, 'head'), may hold values from -0.5 to 0.5
- w_fx: bfloat16 [2, 128, 128], P(None, None, 'head'), may hold values from -0.5 to 0.5
- w_slice: bfloat16 [2, 32, 32], replicated
- temper: float32 [2, 4], replicated, may hold values from 0.5 to 2
- query_weight: bfloat16 [2, 32, 32], replicated
- key_weight: bfloat16 [2, 32, 32], replicated, may hold values from -1 to 1
- value_weight: bfloat16 [2, 32, 32], replicated, may hold values from -1 to 1
- w_out: bfloat16 [2, 128, 128], P(None, 'head'), may hold values from -1 to 1
- b_out: float32 [2, 128], replicated, may hold values from -1.5 to 1.5
- ln2_gain: float32 [2, 128], replicated, may hold values from 0.5 to 1.5
- ln2_bias: float32 [2, 128], replicated, may hold values from -1.5 to 1.5
- w_up: bfloat16 [2, 128, 512], replicated, may hold values from -0.5 to 0.5
- w_down: bfloat16 [2, 512, 128], replicated, may hold values from -0.25 to 0.25
Outputs:
- features: bfloat16 [73728, 128], P(('pts', 'head'))
Inputs may be any that keep to these rules, and one draw needn't show every extreme that they name: counts[i] live points fill the first slots of shard i; at least one shard is full; they sum to 55296.
All inputs are finite; a program needn't handle non-finite values.
Results may differ from a plain program's by a relative error of at most 0.014.
Values may be sent and summed in bfloat16 or wider, within the bound.
A program may use at most 128 MiB of HBM per device.

v0:
```python
import jax
import jax.numpy as jnp
from jax import lax
from jax.sharding import PartitionSpec as P

DH = 32
M = 32


def layer_norm(value, gain, bias):
    mean = jnp.mean(value, axis=-1, keepdims=True)
    centred = value - mean
    var = jnp.mean(centred * centred, axis=-1, keepdims=True)
    return centred * lax.rsqrt(var + 1e-05) * gain + bias


def slice_attention(token_rows, query_weight, key_weight, value_weight):
    head_parts = lax.Precision.HIGHEST
    query_rows = jnp.einsum(
        "aur,rz->auz", token_rows, query_weight.astype(jnp.float32), precision=head_parts
    )
    slice_keys = jnp.einsum(
        "aur,rz->auz", token_rows, key_weight.astype(jnp.float32), precision=head_parts
    )
    slice_values = jnp.einsum(
        "aur,rz->auz", token_rows, value_weight.astype(jnp.float32), precision=head_parts
    )
    scores = jnp.einsum("hme,hke->hmk", query_rows, slice_keys, precision=head_parts) * DH ** (-0.5)
    attn = jax.nn.softmax(scores, axis=-1)
    return jnp.einsum("hmk,hke->hme", attn, slice_values, precision=head_parts).astype(jnp.bfloat16)


def body(
    points,
    counts,
    ln1_gain,
    ln1_bias,
    w_in,
    w_fx,
    w_slice,
    temper,
    query_weight,
    key_weight,
    value_weight,
    w_out,
    b_out,
    ln2_gain,
    ln2_bias,
    w_up,
    w_down,
):
    groups = lax.axis_size("head")
    rows = points.shape[0] // groups
    first_row = lax.axis_index("head") * rows
    layers = w_in.shape[0]
    full_in = lax.all_gather(w_in, "head", axis=2, tiled=True)
    full_fx = lax.all_gather(w_fx, "head", axis=2, tiled=True)
    full_out = lax.all_gather(w_out, "head", axis=1, tiled=True)
    heads = full_in.shape[2] // DH
    live = (first_row + jnp.arange(rows, dtype=jnp.int32) < counts[0]).astype(jnp.float32)
    current = lax.dynamic_slice_in_dim(points, first_row, rows, 0)
    for layer_index in range(layers):
        normed = layer_norm(
            current.astype(jnp.float32), ln1_gain[layer_index], ln1_bias[layer_index]
        ).astype(jnp.bfloat16)
        mid = jnp.dot(normed, full_in[layer_index], preferred_element_type=jnp.float32).astype(
            jnp.bfloat16
        )
        feats = jnp.dot(normed, full_fx[layer_index], preferred_element_type=jnp.float32).astype(
            jnp.bfloat16
        )
        spread = jnp.kron(jnp.eye(heads, dtype=jnp.bfloat16), w_slice[layer_index])
        logits = jnp.dot(mid, spread, preferred_element_type=jnp.float32)
        logits = logits.reshape(rows, heads, M) / temper[layer_index][None, :, None]
        weights = jax.nn.softmax(logits, axis=-1) * live[:, None, None]
        half_weights = weights.astype(jnp.bfloat16).reshape(rows, heads * M)
        total = jnp.sum(weights, axis=0)
        square = jnp.einsum("rs,rl->sl", half_weights, feats, preferred_element_type=jnp.float32)
        square = square.reshape(heads, M, heads, DH)
        numerator = jnp.stack([square[h, :, h, :] for h in range(heads)])
        numerator, total = lax.psum((numerator, total), ("pts", "head"))
        token_rows = numerator / jnp.maximum(total, 1.0)[..., None]
        mixed_token = slice_attention(
            token_rows,
            query_weight[layer_index],
            key_weight[layer_index],
            value_weight[layer_index],
        )
        wide = (
            jnp.einsum(
                "hmv,hvc->hmc",
                mixed_token,
                full_out[layer_index].reshape(heads, DH, -1),
                preferred_element_type=jnp.float32,
            )
            .astype(jnp.bfloat16)
            .reshape(heads * M, -1)
        )
        projected = jnp.dot(half_weights, wide, preferred_element_type=jnp.float32)
        after = current.astype(jnp.float32) + projected + b_out[layer_index]
        normed2 = layer_norm(after, ln2_gain[layer_index], ln2_bias[layer_index]).astype(
            jnp.bfloat16
        )
        upper = jax.nn.gelu(
            jnp.dot(normed2, w_up[layer_index], preferred_element_type=jnp.float32)
        ).astype(jnp.bfloat16)
        current = (
            after + jnp.dot(upper, w_down[layer_index], preferred_element_type=jnp.float32)
        ).astype(jnp.bfloat16)
    return current


def solution(mesh):
    placed = (
        P("pts", None),
        P("pts"),
        P(),
        P(),
        P(None, None, "head"),
        P(None, None, "head"),
        P(),
        P(),
        P(),
        P(),
        P(),
        P(None, "head", None),
        P(),
        P(),
        P(),
        P(),
        P(),
    )
    return jax.shard_map(
        body, mesh=mesh, in_specs=placed, out_specs=P(("pts", "head"), None), check_vma=False
    )
```

profile of v0, /device:TPU:0, one launch (start us, length us, event | category | flops | bytes accessed | tf_op | source)
XLA Modules:
  0.0 157.5 jit_solution(5383199505180625222)
XLA Ops:
  0.0 1.7 %copy-done = bf16[9216,128]{1,0:T(8,128)(2,1)S(1)} copy-done((bf16[9216,128]{1,0:T(8,128)(2,1)S(1)}, bf16[9216,128]{1,0:T(8,128)(2,1)}, u32[]{:S(2)}) %copy-start) | copy-done | bytes 2359320
  1.7 0.2 copy.26
  2.1 0.2 fusion.33
  2.3 0.3 copy-done.18
  2.7 0.6 slice_bitcast_fusion.34
  3.5 0.8 broadcast_multiply_fusion
  4.4 9.7 %all_gather.9 = bf16[2,128,128]{1,2,0:T(8,128)(2,1)S(1)} all-gather(bf16[2,128,32]{1,2,0:T(8,128)(2,1)S(1)} %copy-done.10), channel_id=1, replica_groups=mesh['pts'=8,'head'=4] {'head'}, dimensions={2}, use_global_device_ids=true | all-gather | bytes 81920 | tf_op jit(solution)/shard_map/all_gather | solution.py:56
  14.2 1.9 %fusion.122 = (f32[2304,4]{0,1:T(4,128)S(1)}, f32[2304,4,32]{0,2,1:T(8,128)}) fusion(bf16[4,32,128]{2,1,0:T(8,128)(2,1)S(1)} %bitcast.209, f32[4]{0:T(128)S(1)} %get-tuple-element.28, bf16[2,128,128]{1,2,0:T(8,128)(2,1)S(1)} %all_gather.9, bf16[2304,128]{0,1:T(8,128)(2,1)S(1)} %copy.26, f32[128]{0:T(128)S(1)} %get-tuple-element.34, ...), kind=kOutput, calls=%fused_computation.175 | convolution fusion | flops 153944096 | bytes 1897984 | tf_op jit(solution)/shard_map/sub | solution.py:75
  16.7 1.6 %fusion.57 = f32[4,32]{1,0:T(4,128)S(1)} fusion(f32[2304]{0:T(1024)S(1)} %fusion.83, f32[2304,4,32]{0,2,1:T(8,128)} %get-tuple-element.36, f32[2304,4]{0,1:T(4,128)S(1)} %get-tuple-element.35), kind=kLoop, calls=%fused_computation.77 | loop fusion | flops 884608 | bytes 1226240 | tf_op jit(solution)/shard_map/reduce_sum | solution.py:77
  18.3 8.2 %all_gather.10 = bf16[2,128,128]{1,2,0:T(8,128)(2,1)S(1)} all-gather(bf16[2,128,32]{1,2,0:T(8,128)(2,1)S(1)} %copy-done.11), channel_id=1, replica_groups=mesh['pts'=8,'head'=4] {'head'}, dimensions={2}, use_global_device_ids=true | all-gather | bytes 81920 | tf_op jit(solution)/shard_map/all_gather | solution.py:57
  26.5 0.4 convolution_convert_fusion.1
  27.0 0.6 fusion.39
  27.7 40.2 %all-reduce.1 = (f32[4,32,32]{2,1,0:T(8,128)S(1)}, f32[4,32]{1,0:T(4,128)S(1)}) all-reduce(f32[4,32,32]{2,1,0:T(8,128)S(1)} %pad_maximum_fusion, f32[4,32]{1,0:T(4,128)S(1)} %fusion.57), channel_id=1, replica_groups=mesh['pts'=8,'head'=4] {'pts','head'}, use_global_device_ids=true, to_apply=%region_4.5 | all-reduce | flops 4224 | bytes 33792 | tf_op jit(solution)/shard_map/psum | solution.py:81
  67.9 0.2 fusion.92
  68.2 0.2 fusion.94
  68.4 0.2 fusion.125
  68.7 0.2 fusion.90
  69.0 0.3 convolution_convert_fusion.7
  69.3 9.0 %all_gather.11 = bf16[2,128,128]{2,1,0:T(8,128)(2,1)S(1)} all-gather(bf16[2,32,128]{2,1,0:T(8,128)(2,1)S(1)} %copy-done.12), channel_id=1, replica_groups=mesh['pts'=8,'head'=4] {'head'}, dimensions={1}, use_global_device_ids=true | all-gather | bytes 81920 | tf_op jit(solution)/shard_map/all_gather | solution.py:58
  78.3 0.6 fusion.121
  78.9 0.5 slice_bitcast_fusion.32
  79.4 2.8 %fusion.126 = (f32[2304]{0:T(1024)S(1)}, f32[2304,128]{0,1:T(8,128)}) fusion(f32[128]{0:T(128)S(1)} %get-tuple-element.26, bf16[4,32,32]{2,1,0:T(8,128)(2,1)S(1)} %convolution_convert_fusion.7, bf16[4,32,128]{2,1,0:T(8,128)(2,1)S(1)} %bitcast.212, f32[2304]{0:T(1024)S(1)} %fusion.83, f32[2304,4,32]{0,2,1:T(8,128)} %get-tuple-element.36, ...), kind=kOutput, calls=%fused_computation.177 | convolution fusion | flops 78624512 | bytes 3045888 | tf_op jit(solution)/shard_map/dot_general | solution.py:99
  82.2 1.4 multiply_reduce_fusion.2
  83.6 0.6 add_rsqrt_fusion.2
  84.2 0.6 slice_bitcast_fusion.30
  84.8 4.6 %fusion.127 = (f32[2304]{0:T(1024)}, f32[2304,128]{0,1:T(8,128)S(1)}) fusion(f32[2304,128]{0,1:T(8,128)} %get-tuple-element.40, bf16[2,512,128]{2,1,0:T(8,128)(2,1)} %param.33, f32[128]{0:T(128)} %get-tuple-element.24, f32[128]{0:T(128)} %get-tuple-element.51, f32[2304]{0:T(1024)} %add_rsqrt_fusion.2, f32[2304]{0:T(1024)} %copy-done.8, ...), kind=kOutput, calls=%fused_computation.178 | convolution fusion | flops 617248512 | bytes 3835904 | tf_op jit(solution)/shard_map/dot_general | solution.py:108
  89.4 0.7 broadcast_multiply_fusion.3
  90.1 0.1 multiply_reduce_fusion.1
  90.3 1.2 add_convert_fusion.1
  91.5 1.6 %mul.210 = bf16[128,128]{0,1:T(8,128)(2,1)} reshape(bf16[4,32,4,32]{1,0,3,2:T(4,128)(2,1)} %get-tuple-element.29) | data formatting | bytes 65536 | tf_op jit(solution)/shard_map/jit(kron)/mul | solution.py:72
  93.1 3.4 %fusion.130 = (f32[2304,4]{0,1:T(4,128)}, f32[2304,4,32]{0,2,1:T(8,128)}) fusion(bf16[4,32,128]{2,1,0:T(8,128)(2,1)} %bitcast.210, bf16[2304,128]{0,1:T(8,128)(2,1)} %add_convert_fusion.1, f32[4]{0:T(128)S(1)} %get-tuple-element.27, bf16[2,128,128]{1,2,0:T(8,128)(2,1)} %copy-done.7), kind=kOutput, calls=%fused_computation.179 | convolution fusion | flops 152174624 | bytes 1871888 | tf_op jit(solution)/shard_map/sub | solution.py:75
  96.5 1.6 %fusion.59 = f32[4,32]{1,0:T(4,128)S(1)} fusion(f32[2304]{0:T(1024)S(1)} %fusion.83, f32[2304,4,32]{0,2,1:T(8,128)} %get-tuple-element.44, f32[2304,4]{0,1:T(4,128)} %get-tuple-element.43), kind=kLoop, calls=%fused_computation.79 | loop fusion | flops 884608 | bytes 1226240 | tf_op jit(solution)/shard_map/reduce_sum | solution.py:77
  98.2 0.3 convolution_convert_fusion
  98.5 0.6 fusion.37
  99.1 0.6 pad_maximum_fusion.1
  99.7 40.3 %all-reduce = (f32[4,32,32]{2,1,0:T(8,128)}, f32[4,32]{1,0:T(4,128)}) all-reduce(f32[4,32,32]{2,1,0:T(8,128)} %pad_maximum_fusion.1, f32[4,32]{1,0:T(4,128)S(1)} %fusion.59), channel_id=1, replica_groups=mesh['pts'=8,'head'=4] {'pts','head'}, use_global_device_ids=true, to_apply=%region_15.16 | all-reduce | flops 4224 | bytes 33792 | tf_op jit(solution)/shard_map/psum | solution.py:81
  140.0 0.7 broadcast_maximum_fusion
  140.7 1.1 fusion.86
  141.8 1.1 fusion.88
  142.9 0.2 fusion.131
  143.1 1.1 fusion.84
  144.2 0.9 convolution_convert_fusion.5
  145.2 3.4 %fusion.132 = (f32[2304]{0:T(1024)}, f32[2304,128]{0,1:T(8,128)}) fusion(f32[128]{0:T(128)} %get-tuple-element.25, f32[2304,128]{0,1:T(8,128)S(1)} %get-tuple-element.42, bf16[4,32,32]{2,1,0:T(8,128)(2,1)} %convolution_convert_fusion.5, bf16[4,32,128]{2,1,0:T(8,128)(2,1)} %bitcast.211, f32[2304]{0:T(1024)S(1)} %fusion.83, ...), kind=kOutput, calls=%fused_computation.181 | convolution fusion | flops 78329600 | bytes 3635712 | tf_op jit(solution)/shard_map/dot_general | solution.py:99
  148.6 0.8 broadcast_multiply_fusion.2
  149.4 1.4 multiply_reduce_fusion
  150.8 0.6 add_rsqrt_fusion
  151.4 4.0 %fusion.27 = bf16[2304,128]{0,1:T(8,128)(2,1)} fusion(f32[2304,128]{0,1:T(8,128)S(1)} %copy-done.4, f32[128]{0:T(128)S(1)} %copy-done.22, f32[128]{0:T(128)} %get-tuple-element.52, f32[2304]{0:T(1024)} %add_rsqrt_fusion, f32[2304]{0:T(1024)S(1)} %broadcast_multiply_fusion.2, bf16[2,512,128]{2,1,0:T(8,128)(2,1)} %param.33, bf16[2,128,512]{2,1,0:T(8,128)(2,1)} %param.32), kind=kOutput, calls=%fused_computation.35 | convolution fusion | flops 616660992 | bytes 3236864 | tf_op jit(solution)/shard_map/dot_general | solution.py:108
  155.4 2.1 %copy.22 = bf16[2304,128]{1,0:T(8,128)(2,1)} copy(bf16[2304,128]{0,1:T(8,128)(2,1)} %fusion.27) | data formatting | bytes 1179648 | tf_op jit(solution)/shard_map/convert_element_type | solution.py:109
  (69 shorter events, 0.7 us)
Async XLA Ops:
  0.0 1.7 %copy-start = (bf16[9216,128]{1,0:T(8,128)(2,1)S(1)}, bf16[9216,128]{1,0:T(8,128)(2,1)}, u32[]{:S(2)}) copy-start(bf16[9216,128]{1,0:T(8,128)(2,1)} %param.17) | copy-start | bytes 7077892
  1.7 1.6 copy-start.13
  2.0 0.7 copy-start.18
  2.0 0.7 copy-start.19
  2.0 2.4 %copy-start.10 = (bf16[2,128,32]{1,2,0:T(8,128)(2,1)S(1)}, bf16[2,128,32]{1,2,0:T(8,128)(2,1)}, u32[]{:S(2)}) copy-start(bf16[2,128,32]{1,2,0:T(8,128)(2,1)} %param.21) | copy-start | bytes 49156
  2.0 12.1 %copy-start.16 = (f32[2,4]{1,0:T(2,128)S(1)}, f32[2,4]{1,0:T(2,128)}, u32[]{:S(2)}) copy-start(f32[2,4]{1,0:T(2,128)} %param.24) | copy-start | bytes 100
  14.1 1.9 %copy-start.7 = (bf16[2,128,128]{1,2,0:T(8,128)(2,1)}, bf16[2,128,128]{1,2,0:T(8,128)(2,1)S(1)}, u32[]{:S(2)}) copy-start(bf16[2,128,128]{1,2,0:T(8,128)(2,1)S(1)} %all_gather.9) | copy-start | bytes 196612
  16.0 2.3 %copy-start.11 = (bf16[2,128,32]{1,2,0:T(8,128)(2,1)S(1)}, bf16[2,128,32]{1,2,0:T(8,128)(2,1)}, u32[]{:S(2)}) copy-start(bf16[2,128,32]{1,2,0:T(8,128)(2,1)} %param.22) | copy-start | bytes 49156
  16.7 10.3 %copy-start.2 = (f32[2304,4,32]{0,2,1:T(8,128)S(1)}, f32[2304,4,32]{0,2,1:T(8,128)}, u32[]{:S(2)}) copy-start(f32[2304,4,32]{0,2,1:T(8,128)} %get-tuple-element.36) | copy-start | bytes 3538948
  26.5 1.1 copy-start.5
  27.0 40.9 %copy-start.23 = (bf16[2,32,32]{2,1,0:T(8,128)(2,1)S(1)}, bf16[2,32,32]{2,1,0:T(8,128)(2,1)}, u32[]{:S(2)}) copy-start(bf16[2,32,32]{2,1,0:T(8,128)(2,1)} %param.26) | copy-start | bytes 12292
  27.0 41.2 %copy-start.24 = (bf16[2,32,32]{2,1,0:T(8,128)(2,1)S(1)}, bf16[2,32,32]{2,1,0:T(8,128)(2,1)}, u32[]{:S(2)}) copy-start(bf16[2,32,32]{2,1,0:T(8,128)(2,1)} %param.25) | copy-start | bytes 12292
  27.0 41.7 %copy-start.25 = (bf16[2,32,32]{2,1,0:T(8,128)(2,1)S(1)}, bf16[2,32,32]{2,1,0:T(8,128)(2,1)}, u32[]{:S(2)}) copy-start(bf16[2,32,32]{2,1,0:T(8,128)(2,1)} %param.27) | copy-start | bytes 12292
  27.6 41.6 %copy-start.12 = (bf16[2,32,128]{2,1,0:T(8,128)(2,1)S(1)}, bf16[2,32,128]{2,1,0:T(8,128)(2,1)}, u32[]{:S(2)}) copy-start(bf16[2,32,128]{2,1,0:T(8,128)(2,1)} %param.28) | copy-start | bytes 49156
  27.6 51.2 %copy-start.17 = (f32[2,128]{1,0:T(2,128)S(1)}, f32[2,128]{1,0:T(2,128)}, u32[]{:S(2)}) copy-start(f32[2,128]{1,0:T(2,128)} %param.29) | copy-start | bytes 3076
  82.2 2.1 %copy-start.20 = (f32[2,128]{1,0:T(2,128)S(1)}, f32[2,128]{1,0:T(2,128)}, u32[]{:S(2)}) copy-start(f32[2,128]{1,0:T(2,128)} %param.31) | copy-start | bytes 3076
  82.2 2.1 %copy-start.21 = (f32[2,128]{1,0:T(2,128)S(1)}, f32[2,128]{1,0:T(2,128)}, u32[]{:S(2)}) copy-start(f32[2,128]{1,0:T(2,128)} %param.30) | copy-start | bytes 3076
  82.2 2.7 %copy-start.8 = (f32[2304]{0:T(1024)}, f32[2304]{0:T(1024)S(1)}, u32[]{:S(2)}) copy-start(f32[2304]{0:T(1024)S(1)} %broadcast_multiply_fusion.4) | copy-start | bytes 27652
  89.4 0.9 copy-start.14
  89.4 0.9 copy-start.15
  96.5 1.6 %copy-start.1 = (bf16[2304,128]{0,1:T(8,128)(2,1)S(1)}, bf16[2304,128]{0,1:T(8,128)(2,1)}, u32[]{:S(2)}) copy-start(bf16[2304,128]{0,1:T(8,128)(2,1)} %add_convert_fusion.1) | copy-start | bytes 1769476
  96.5 1.6 %copy-start.6 = (bf16[2,128,128]{1,2,0:T(8,128)(2,1)S(1)}, bf16[2,128,128]{1,2,0:T(8,128)(2,1)}, u32[]{:S(2)}) copy-start(bf16[2,128,128]{1,2,0:T(8,128)(2,1)} %copy-done.5) | copy-start | bytes 196612
  96.5 2.0 %copy-start.3 = (f32[2304,4,32]{0,2,1:T(8,128)S(1)}, f32[2304,4,32]{0,2,1:T(8,128)}, u32[]{:S(2)}) copy-start(f32[2304,4,32]{0,2,1:T(8,128)} %get-tuple-element.44) | copy-start | bytes 3538948
  96.5 2.0 %copy-start.9 = (f32[2304,4]{0,1:T(4,128)S(1)}, f32[2304,4]{0,1:T(4,128)}, u32[]{:S(2)}) copy-start(f32[2304,4]{0,1:T(4,128)} %get-tuple-element.43) | copy-start | bytes 110596
  148.6 2.8 %copy-start.4 = (f32[2304,128]{0,1:T(8,128)S(1)}, f32[2304,128]{0,1:T(8,128)}, u32[]{:S(2)}) copy-start(f32[2304,128]{0,1:T(8,128)} %get-tuple-element.48) | copy-start | bytes 3538948
  148.6 2.8 %copy-start.22 = (f32[128]{0:T(128)S(1)}, f32[128]{0:T(128)}, u32[]{:S(2)}) copy-start(f32[128]{0:T(128)} %get-tuple-element.23) | copy-start | bytes 1540
where the time goes:
time: 159 us; the launch traced here: 158 us
  blocking collectives  107 us (67%)
  matrix products  27.6 us (17%)
  other arithmetic  12.6 us (8%)
  local copies, waits for them, and re-layouts  8.79 us (6%)
    psum x2, blocking collectives, body(): numerator, total = lax.psum((numerator, total), ('pts', 'head'))  80.5 us
    all_gather x1, blocking collectives, body(): full_in = lax.all_gather(w_in, 'head', axis=2, tiled=True)  9.72 us
    all_gather x1, blocking collectives, body(): full_out = lax.all_gather(w_out, 'head', axis=1, tiled=True)  9 us
    dot_general x2, matrix products, body(): jnp.dot(upper, w_down[layer_index], preferred_element_type=jnp.float32)  8.51 us
    all_gather x1, blocking collectives, body(): full_fx = lax.all_gather(w_fx, 'head', axis=2, tiled=True)  8.21 us
    dot_general x2, matrix products, body(): projected = jnp.dot(half_weights, wide, preferred_element_type=jnp.float32)  6.22 us
    sub x2, matrix products, body(): weights = jax.nn.softmax(logits, axis=-1) * live[:, None, None]  5.29 us
    reduce_sum x2, other arithmetic, body(): total = jnp.sum(weights, axis=0)  3.22 us

commit v1 on v0

--- a/solution.py
+++ b/solution.py
@@ -78,7 +78,7 @@
         square = jnp.einsum("rs,rl->sl", half_weights, feats, preferred_element_type=jnp.float32)
         square = square.reshape(heads, M, heads, DH)
         numerator = jnp.stack([square[h, :, h, :] for h in range(heads)])
-        numerator, total = lax.psum((numerator, total), ("pts", "head"))
+        numerator, total = lax.psum(lax.psum((numerator, total), "head"), "pts")
         token_rows = numerator / jnp.maximum(total, 1.0)[..., None]
         mixed_token = slice_attention(
             token_rows,

time: 159 us -> 164 us (1.031)
  blocking collectives: 107 us -> 114 us
    psum x2 -> x4, blocking collectives: 80.5 us -> 88.7 us  [body(): numerator, total = lax.psum(lax.psum((numerator, total), 'head'), 'pts')]
    all_gather x1, blocking collectives: 9 us -> 7.34 us  [body(): full_out = lax.all_gather(w_out, 'head', axis=1, tiled=True)]
where the time goes in v1:
time: 164 us; the launch traced here: 163 us
  blocking collectives  114 us (70%)
  matrix products  27.6 us (17%)
  other arithmetic  12 us (7%)
  local copies, waits for them, and re-layouts  8.79 us (5%)
    psum x4, blocking collectives, body(): numerator, total = lax.psum(lax.psum((numerator, total), 'head'), 'pts')  88.7 us
    all_gather x1, blocking collectives, body(): full_in = lax.all_gather(w_in, 'head', axis=2, tiled=True)  9.72 us
    dot_general x2, matrix products, body(): jnp.dot(upper, w_down[layer_index], preferred_element_type=jnp.float32)  8.51 us
    all_gather x1, blocking collectives, body(): full_fx = lax.all_gather(w_fx, 'head', axis=2, tiled=True)  8.21 us
    all_gather x1, blocking collectives, body(): full_out = lax.all_gather(w_out, 'head', axis=1, tiled=True)  7.34 us
    dot_general x2, matrix products, body(): projected = jnp.dot(half_weights, wide, preferred_element_type=jnp.float32)  6.22 us
    sub x2, matrix products, body(): weights = jax.nn.softmax(logits, axis=-1) * live[:, None, None]  5.29 us

profile of v1, /device:TPU:0, one launch (start us, length us, event | category | flops | bytes accessed | tf_op | source)
XLA Modules:
  0.0 163.4 jit_solution(9723353268955519072)
XLA Ops:
  0.0 1.7 %copy-done = bf16[9216,128]{1,0:T(8,128)(2,1)S(1)} copy-done((bf16[9216,128]{1,0:T(8,128)(2,1)S(1)}, bf16[9216,128]{1,0:T(8,128)(2,1)}, u32[]{:S(2)}) %copy-start) | copy-done | bytes 2359320
  1.7 0.2 copy.26
  2.1 0.2 fusion.33
  2.3 0.3 copy-done.18
  2.7 0.6 slice_bitcast_fusion.34
  3.5 0.8 broadcast_multiply_fusion
  4.4 9.7 %all_gather.9 = bf16[2,128,128]{1,2,0:T(8,128)(2,1)S(1)} all-gather(bf16[2,128,32]{1,2,0:T(8,128)(2,1)S(1)} %copy-done.10), channel_id=1, replica_groups=mesh['pts'=8,'head'=4] {'head'}, dimensions={2}, use_global_device_ids=true | all-gather | bytes 81920 | tf_op jit(solution)/shard_map/all_gather | solution.py:56
  14.2 1.9 %fusion.122 = (f32[2304,4]{0,1:T(4,128)S(1)}, f32[2304,4,32]{0,2,1:T(8,128)}) fusion(bf16[4,32,128]{2,1,0:T(8,128)(2,1)S(1)} %bitcast.209, f32[4]{0:T(128)S(1)} %get-tuple-element.32, bf16[2,128,128]{1,2,0:T(8,128)(2,1)S(1)} %all_gather.9, bf16[2304,128]{0,1:T(8,128)(2,1)S(1)} %copy.26, f32[128]{0:T(128)S(1)} %get-tuple-element.38, ...), kind=kOutput, calls=%fused_computation.175 | convolution fusion | flops 153944096 | bytes 1897984 | tf_op jit(solution)/shard_map/sub | solution.py:75
  16.7 1.6 fusion.57
  18.3 8.2 %all_gather.10 = bf16[2,128,128]{1,2,0:T(8,128)(2,1)S(1)} all-gather(bf16[2,128,32]{1,2,0:T(8,128)(2,1)S(1)} %copy-done.11), channel_id=1, replica_groups=mesh['pts'=8,'head'=4] {'head'}, dimensions={2}, use_global_device_ids=true | all-gather | bytes 81920 | tf_op jit(solution)/shard_map/all_gather | solution.py:57
  26.5 0.4 convolution_convert_fusion.1
  27.0 0.6 fusion.39
  27.7 16.5 %all-reduce.3 = (f32[4,32,32]{2,1,0:T(8,128)S(1)}, f32[4,32]{1,0:T(4,128)S(1)}) all-reduce(f32[4,32,32]{2,1,0:T(8,128)S(1)} %pad_maximum_fusion, f32[4,32]{1,0:T(4,128)S(1)} %fusion.57), channel_id=1, replica_groups=mesh['pts'=8,'head'=4] {'head'}, use_global_device_ids=true, to_apply=%region_4.5 | all-reduce | flops 4224 | bytes 33792 | tf_op jit(solution)/shard_map/psum | solution.py:81
  44.2 26.8 %all-reduce.1 = (f32[4,32,32]{2,1,0:T(8,128)S(1)}, f32[4,32]{1,0:T(4,128)S(1)}) all-reduce(f32[4,32,32]{2,1,0:T(8,128)S(1)} %get-tuple-element.11, f32[4,32]{1,0:T(4,128)S(1)} %get-tuple-element.12), channel_id=1, replica_groups=mesh['pts'=8,'head'=4] {'pts'}, use_global_device_ids=true, to_apply=%region_5.6 | all-reduce | flops 4224 | bytes 33792 | tf_op jit(solution)/shard_map/psum | solution.py:81
  71.1 0.2 fusion.92
  71.3 0.2 fusion.94
  71.6 0.2 fusion.125
  71.9 0.2 fusion.90
  72.1 0.3 convolution_convert_fusion.7
  72.4 7.3 %all_gather.11 = bf16[2,128,128]{2,1,0:T(8,128)(2,1)S(1)} all-gather(bf16[2,32,128]{2,1,0:T(8,128)(2,1)S(1)} %copy-done.12), channel_id=1, replica_groups=mesh['pts'=8,'head'=4] {'head'}, dimensions={1}, use_global_device_ids=true | all-gather | bytes 81920 | tf_op jit(solution)/shard_map/all_gather | solution.py:58
  79.8 0.6 fusion.121
  80.4 0.5 slice_bitcast_fusion.32
  80.9 2.8 %fusion.126 = (f32[2304]{0:T(1024)S(1)}, f32[2304,128]{0,1:T(8,128)}) fusion(f32[128]{0:T(128)S(1)} %get-tuple-element.30, bf16[4,32,32]{2,1,0:T(8,128)(2,1)S(1)} %convolution_convert_fusion.7, bf16[4,32,128]{2,1,0:T(8,128)(2,1)S(1)} %bitcast.212, f32[2304]{0:T(1024)S(1)} %fusion.83, f32[2304,4,32]{0,2,1:T(8,128)} %get-tuple-element.40, ...), kind=kOutput, calls=%fused_computation.177 | convolution fusion | flops 78624512 | bytes 3045888 | tf_op jit(solution)/shard_map/dot_general | solution.py:99
  83.7 1.4 multiply_reduce_fusion.2
  85.1 0.6 add_rsqrt_fusion.2
  85.7 0.6 slice_bitcast_fusion.30
  86.3 4.5 %fusion.127 = (f32[2304]{0:T(1024)}, f32[2304,128]{0,1:T(8,128)S(1)}) fusion(f32[2304,128]{0,1:T(8,128)} %get-tuple-element.44, bf16[2,512,128]{2,1,0:T(8,128)(2,1)} %param.33, f32[128]{0:T(128)} %get-tuple-element.28, f32[128]{0:T(128)} %get-tuple-element.55, f32[2304]{0:T(1024)} %add_rsqrt_fusion.2, f32[2304]{0:T(1024)} %copy-done.8, ...), kind=kOutput, calls=%fused_computation.178 | convolution fusion | flops 617248512 | bytes 3835904 | tf_op jit(solution)/shard_map/dot_general | solution.py:108
  90.9 0.7 broadcast_multiply_fusion.3
  91.8 1.2 add_convert_fusion.1
  93.0 1.6 %mul.210 = bf16[128,128]{0,1:T(8,128)(2,1)} reshape(bf16[4,32,4,32]{1,0,3,2:T(4,128)(2,1)} %get-tuple-element.33) | data formatting | bytes 65536 | tf_op jit(solution)/shard_map/jit(kron)/mul | solution.py:72
  94.6 3.4 %fusion.130 = (f32[2304,4]{0,1:T(4,128)}, f32[2304,4,32]{0,2,1:T(8,128)}) fusion(bf16[4,32,128]{2,1,0:T(8,128)(2,1)} %bitcast.210, bf16[2304,128]{0,1:T(8,128)(2,1)} %add_convert_fusion.1, f32[4]{0:T(128)S(1)} %get-tuple-element.31, bf16[2,128,128]{1,2,0:T(8,128)(2,1)} %copy-done.7), kind=kOutput, calls=%fused_computation.179 | convolution fusion | flops 152174624 | bytes 1871888 | tf_op jit(solution)/shard_map/sub | solution.py:75
  98.0 1.6 fusion.59
  99.7 0.3 convolution_convert_fusion
  100.0 0.6 fusion.37
  100.6 0.6 pad_maximum_fusion.1
  101.2 17.4 %all-reduce.2 = (f32[4,32,32]{2,1,0:T(8,128)}, f32[4,32]{1,0:T(4,128)}) all-reduce(f32[4,32,32]{2,1,0:T(8,128)} %pad_maximum_fusion.1, f32[4,32]{1,0:T(4,128)S(1)} %fusion.59), channel_id=1, replica_groups=mesh['pts'=8,'head'=4] {'head'}, use_global_device_ids=true, to_apply=%region_17.18 | all-reduce | flops 4224 | bytes 33792 | tf_op jit(solution)/shard_map/psum | solution.py:81
  118.6 28.0 %all-reduce = (f32[4,32,32]{2,1,0:T(8,128)}, f32[4,32]{1,0:T(4,128)S(1)}) all-reduce(f32[4,32,32]{2,1,0:T(8,128)} %get-tuple-element.9, f32[4,32]{1,0:T(4,128)} %get-tuple-element.10), channel_id=1, replica_groups=mesh['pts'=8,'head'=4] {'pts'}, use_global_device_ids=true, to_apply=%region_18.19 | all-reduce | flops 4224 | bytes 33792 | tf_op jit(solution)/shard_map/psum | solution.py:81
  146.6 1.1 fusion.86
  147.7 1.1 fusion.88
  148.8 0.2 fusion.131
  149.1 1.1 fusion.84
  150.2 0.9 convolution_convert_fusion.5
  151.1 3.4 %fusion.132 = (f32[2304]{0:T(1024)}, f32[2304,128]{0,1:T(8,128)}) fusion(f32[128]{0:T(128)} %get-tuple-element.29, f32[2304,128]{0,1:T(8,128)S(1)} %get-tuple-element.46, bf16[4,32,32]{2,1,0:T(8,128)(2,1)} %convolution_convert_fusion.5, bf16[4,32,128]{2,1,0:T(8,128)(2,1)} %bitcast.211, f32[2304]{0:T(1024)S(1)} %fusion.83, ...), kind=kOutput, calls=%fused_computation.181 | convolution fusion | flops 78329600 | bytes 3635712 | tf_op jit(solution)/shard_map/dot_general | solution.py:99
  154.5 0.8 broadcast_multiply_fusion.2
  155.3 1.4 multiply_reduce_fusion
  156.7 0.6 add_rsqrt_fusion
  157.4 4.0 %fusion.27 = bf16[2304,128]{0,1:T(8,128)(2,1)} fusion(f32[2304,128]{0,1:T(8,128)S(1)} %copy-done.4, f32[128]{0:T(128)S(1)} %copy-done.22, f32[128]{0:T(128)} %get-tuple-element.56, f32[2304]{0:T(1024)} %add_rsqrt_fusion, f32[2304]{0:T(1024)S(1)} %broadcast_multiply_fusion.2, bf16[2,512,128]{2,1,0:T(8,128)(2,1)} %param.33, bf16[2,128,512]{2,1,0:T(8,128)(2,1)} %param.32), kind=kOutput, calls=%fused_computation.35 | convolution fusion | flops 616660992 | bytes 3236864 | tf_op jit(solution)/shard_map/dot_general | solution.py:108
  161.3 2.1 %copy.22 = bf16[2304,128]{1,0:T(8,128)(2,1)} copy(bf16[2304,128]{0,1:T(8,128)(2,1)} %fusion.27) | data formatting | bytes 1179648 | tf_op jit(solution)/shard_map/convert_element_type | solution.py:109
  (71 shorter events, 0.8 us)
Async XLA Ops:
  0.0 1.7 %copy-start = (bf16[9216,128]{1,0:T(8,128)(2,1)S(1)}, bf16[9216,128]{1,0:T(8,128)(2,1)}, u32[]{:S(2)}) copy-start(bf16[9216,128]{1,0:T(8,128)(2,1)} %param.17) | copy-start | bytes 7077892
  1.7 1.6 copy-start.13
  2.0 0.7 copy-start.18
  2.0 0.7 copy-start.19
  2.0 2.4 %copy-start.10 = (bf16[2,128,32]{1,2,0:T(8,128)(2,1)S(1)}, bf16[2,128,32]{1,2,0:T(8,128)(2,1)}, u32[]{:S(2)}) copy-start(bf16[2,128,32]{1,2,0:T(8,128)(2,1)} %param.21) | copy-start | bytes 49156
  2.0 12.1 %copy-start.16 = (f32[2,4]{1,0:T(2,128)S(1)}, f32[2,4]{1,0:T(2,128)}, u32[]{:S(2)}) copy-start(f32[2,4]{1,0:T(2,128)} %param.24) | copy-start | bytes 100
  14.1 1.9 %copy-start.7 = (bf16[2,128,128]{1,2,0:T(8,128)(2,1)}, bf16[2,128,128]{1,2,0:T(8,128)(2,1)S(1)}, u32[]{:S(2)}) copy-start(bf16[2,128,128]{1,2,0:T(8,128)(2,1)S(1)} %all_gather.9) | copy-start | bytes 196612
  16.0 2.3 %copy-start.11 = (bf16[2,128,32]{1,2,0:T(8,128)(2,1)S(1)}, bf16[2,128,32]{1,2,0:T(8,128)(2,1)}, u32[]{:S(2)}) copy-start(bf16[2,128,32]{1,2,0:T(8,128)(2,1)} %param.22) | copy-start | bytes 49156
  16.7 10.3 %copy-start.2 = (f32[2304,4,32]{0,2,1:T(8,128)S(1)}, f32[2304,4,32]{0,2,1:T(8,128)}, u32[]{:S(2)}) copy-start(f32[2304,4,32]{0,2,1:T(8,128)} %get-tuple-element.40) | copy-start | bytes 3538948
  26.5 1.1 copy-start.5
  27.0 44.1 %copy-start.23 = (bf16[2,32,32]{2,1,0:T(8,128)(2,1)S(1)}, bf16[2,32,32]{2,1,0:T(8,128)(2,1)}, u32[]{:S(2)}) copy-start(bf16[2,32,32]{2,1,0:T(8,128)(2,1)} %param.26) | copy-start | bytes 12292
  27.0 44.3 %copy-start.24 = (bf16[2,32,32]{2,1,0:T(8,128)(2,1)S(1)}, bf16[2,32,32]{2,1,0:T(8,128)(2,1)}, u32[]{:S(2)}) copy-start(bf16[2,32,32]{2,1,0:T(8,128)(2,1)} %param.25) | copy-start | bytes 12292
  27.0 44.8 %copy-start.25 = (bf16[2,32,32]{2,1,0:T(8,128)(2,1)S(1)}, bf16[2,32,32]{2,1,0:T(8,128)(2,1)}, u32[]{:S(2)}) copy-start(bf16[2,32,32]{2,1,0:T(8,128)(2,1)} %param.27) | copy-start | bytes 12292
  27.6 44.8 %copy-start.12 = (bf16[2,32,128]{2,1,0:T(8,128)(2,1)S(1)}, bf16[2,32,128]{2,1,0:T(8,128)(2,1)}, u32[]{:S(2)}) copy-start(bf16[2,32,128]{2,1,0:T(8,128)(2,1)} %param.28) | copy-start | bytes 49156
  27.6 52.7 %copy-start.17 = (f32[2,128]{1,0:T(2,128)S(1)}, f32[2,128]{1,0:T(2,128)}, u32[]{:S(2)}) copy-start(f32[2,128]{1,0:T(2,128)} %param.29) | copy-start | bytes 3076
  83.7 2.1 %copy-start.20 = (f32[2,128]{1,0:T(2,128)S(1)}, f32[2,128]{1,0:T(2,128)}, u32[]{:S(2)}) copy-start(f32[2,128]{1,0:T(2,128)} %param.31) | copy-start | bytes 3076
  83.7 2.1 %copy-start.21 = (f32[2,128]{1,0:T(2,128)S(1)}, f32[2,128]{1,0:T(2,128)}, u32[]{:S(2)}) copy-start(f32[2,128]{1,0:T(2,128)} %param.30) | copy-start | bytes 3076
  83.7 2.7 %copy-start.8 = (f32[2304]{0:T(1024)}, f32[2304]{0:T(1024)S(1)}, u32[]{:S(2)}) copy-start(f32[2304]{0:T(1024)S(1)} %broadcast_multiply_fusion.4) | copy-start | bytes 27652
  90.9 0.9 copy-start.14
  90.9 0.9 copy-start.15
  98.0 1.6 %copy-start.1 = (bf16[2304,128]{0,1:T(8,128)(2,1)S(1)}, bf16[2304,128]{0,1:T(8,128)(2,1)}, u32[]{:S(2)}) copy-start(bf16[2304,128]{0,1:T(8,128)(2,1)} %add_convert_fusion.1) | copy-start | bytes 1769476
  98.0 1.6 %copy-start.6 = (bf16[2,128,128]{1,2,0:T(8,128)(2,1)S(1)}, bf16[2,128,128]{1,2,0:T(8,128)(2,1)}, u32[]{:S(2)}) copy-start(bf16[2,128,128]{1,2,0:T(8,128)(2,1)} %copy-done.5) | copy-start | bytes 196612
  98.0 2.0 %copy-start.3 = (f32[2304,4,32]{0,2,1:T(8,128)S(1)}, f32[2304,4,32]{0,2,1:T(8,128)}, u32[]{:S(2)}) copy-start(f32[2304,4,32]{0,2,1:T(8,128)} %get-tuple-element.48) | copy-start | bytes 3538948
  98.0 2.0 %copy-start.9 = (f32[2304,4]{0,1:T(4,128)S(1)}, f32[2304,4]{0,1:T(4,128)}, u32[]{:S(2)}) copy-start(f32[2304,4]{0,1:T(4,128)} %get-tuple-element.47) | copy-start | bytes 110596
  154.5 2.8 %copy-start.4 = (f32[2304,128]{0,1:T(8,128)S(1)}, f32[2304,128]{0,1:T(8,128)}, u32[]{:S(2)}) copy-start(f32[2304,128]{0,1:T(8,128)} %get-tuple-element.52) | copy-start | bytes 3538948
  154.5 2.8 %copy-start.22 = (f32[128]{0:T(128)S(1)}, f32[128]{0:T(128)}, u32[]{:S(2)}) copy-start(f32[128]{0:T(128)} %get-tuple-element.27) | copy-start | bytes 1540
